TPU v7x, 32 devices: a whole 2x2x4 slice. The times are simulated.
32 devices in a mesh: genes: 16 (over z, y, core), cols: 2 (over x).
Axes of the slice: x: 2, y: 2, z: 4, core: 2. Of those that a mesh axis runs over, the one named last changes fastest.
Arguments:
- expression: float32 [384, 40960], P(None, ('genes', 'cols')), may hold values from -200 to 200
- resample: int32 [384], replicated, may hold values from 0 to 383
- labels: int32 [40960, 300], P(('genes', 'cols')), may hold values from 0 to 1, as said below
- ref_kim: float32 [40960], P(('genes', 'cols')), may hold values from 0 to 1
Outputs:
- connectivity: float32 [40960, 300], P(('genes', 'cols'))
- preservation: float32 [2, 300], replicated
Inputs may be any that keep to these rules, and one draw needn't show every extreme that they name: `labels`: each row holds exactly one 1; every module has 32 or more genes.
All inputs are finite; a program needn't handle non-finite values.
Results may differ from a plain program's by a relative error of at most 0.0031.
Values may be sent and summed in bfloat16 or wider, within the bound.
A program may use at most 128 MiB of HBM per device.

v0:
```python
import math
import jax
import jax.numpy as jnp
from jax import lax
from jax.sharding import PartitionSpec as P

G = 40960


def standardize(expression, resample):
    boot = jnp.take(expression, resample, axis=0)
    centered = boot - jnp.mean(boot, axis=0, keepdims=True)
    total = jnp.sum(centered * centered, axis=0, keepdims=True)
    return (centered * lax.rsqrt(total + 1e-06)).astype(jnp.bfloat16)


def local_sums(connectivity, labels, ref_kim):
    member = labels.astype(jnp.float32)
    kim = jnp.sum(connectivity * member, axis=1)
    rowsum = jnp.sum(connectivity, axis=1)
    stacked = jnp.stack(
        [kim, kim * kim, ref_kim, ref_kim * ref_kim, kim * ref_kim, rowsum, jnp.ones_like(kim)],
        axis=1,
    )
    return jnp.dot(
        member.T, stacked, precision=lax.Precision.HIGHEST, preferred_element_type=jnp.float32
    )


def preserve(sums, total_genes):
    counts = sums[:, 6]
    mean_x = sums[:, 0] / (counts * counts)
    var_x = jnp.maximum(sums[:, 1] / (counts * counts * counts) - mean_x * mean_x, 0.0001)
    mean_y = sums[:, 2] / counts
    var_y = jnp.maximum(sums[:, 3] / counts - mean_y * mean_y, 0.01)
    cross = sums[:, 4] / (counts * counts) - mean_x * mean_y
    between = (sums[:, 5] - sums[:, 0]) / (counts * (total_genes - counts))
    density = (mean_x - between) * jnp.sqrt(counts / var_x)
    linked = cross * jnp.sqrt(counts / (var_x * var_y))
    return jnp.stack([density, linked], axis=0)


def tile_term(row_block, column_block, column_ids, module_count):
    scores = lax.dot_general(
        row_block, column_block, (((0,), (0,)), ((), ())), preferred_element_type=jnp.float32
    )
    squares = scores * scores
    adjacency = (squares * squares * squares).astype(jnp.bfloat16)
    member_block = (
        column_ids[:, None] == jnp.arange(module_count, dtype=jnp.int32)[None, :]
    ).astype(jnp.bfloat16)
    return jnp.dot(adjacency, member_block, preferred_element_type=jnp.float32)


def add_tiles(carried, row_block, piece, every_ids, shard_width, module_count):
    span_width = piece.shape[1]
    column_step = shard_width * math.gcd(span_width // shard_width, 8)
    steps_total = span_width // column_step

    def one_step(step_index, accumulated):
        columns = lax.dynamic_slice_in_dim(piece, step_index * column_step, column_step, 1)
        column_ids = lax.dynamic_slice_in_dim(every_ids, step_index * column_step, column_step, 0)
        return accumulated + tile_term(row_block, columns, column_ids, module_count)

    return lax.fori_loop(0, steps_total, one_step, carried)


def local(expression, resample, labels, ref_kim):
    scaled = standardize(expression, resample)
    module_count = labels.shape[1]
    shard_width = scaled.shape[1]
    module_ids = jnp.sum(labels * jnp.arange(module_count, dtype=jnp.int32)[None, :], axis=1)
    row_block = lax.all_gather(scaled, "cols", axis=1, tiled=True)
    panel_ids = lax.all_gather(module_ids, "genes", axis=0, tiled=True)
    initial = jnp.zeros((row_block.shape[1], module_count), jnp.float32)
    partial_value = add_tiles(
        initial,
        row_block,
        lax.all_gather(scaled, "genes", axis=1, tiled=True),
        panel_ids,
        shard_width,
        module_count,
    )
    connectivity = lax.psum_scatter(partial_value, "cols", scatter_dimension=0, tiled=True)
    sums = lax.psum(local_sums(connectivity, labels, ref_kim), ("genes", "cols"))
    return (connectivity, preserve(sums, G))


def solution(mesh):
    placed = (P(None, ("genes", "cols")), P(), P(("genes", "cols"), None), P(("genes", "cols")))
    return jax.shard_map(
        local,
        mesh=mesh,
        in_specs=placed,
        out_specs=(P(("genes", "cols"), None), P()),
        check_vma=False,
    )
```

profile of v0, /device:TPU:0, one launch (start us, length us, event | category | flops | bytes accessed | tf_op | source)
XLA Modules:
  0.0 391.7 jit_solution(1327400909456358095)
XLA Ops:
  7.2 0.0 all-gather.6.cloned.1.call-start
  7.2 0.8 compare_select_fusion
  8.0 0.7 compare_and_fusion
  8.8 2.7 gather_fusion
  11.5 1.9 select_reduce_fusion
  13.4 0.2 copy-done.2
  13.6 0.3 multiply_reduce_fusion
  14.0 1.3 multiply_convert_fusion
  15.2 0.0 all-gather.6.cloned.1.call-update
  15.3 0.0 all-gather.4.cloned.1.call-start
  15.3 0.7 all-gather.4.cloned.1.call-update
  16.0 0.0 reduce-scatter.2.cloned.1.call-start
  16.1 0.2 multiply_reduce_fusion.2
  16.3 23.3 %all-gather = s32[16,1,1280]{2,1,0:T(1,128)S(1)} all-gather(s32[1,1,1280]{2,1,0:T(1,128)S(1)} %reshape.229), channel_id=1, replica_groups=mesh['genes'=16,'cols'=2] {'genes'}, dimensions={0}, use_global_device_ids=true | all-gather | bytes 87040 | tf_op jit(solution)/shard_map/all_gather | solution.py:74
  39.6 10.2 %all-gather.6.cloned.1.call-done = bf16[384,2560]{1,0:T(8,128)(2,1)} async-done(((bf16[384,1280]{1,0:T(8,128)(2,1)}), bf16[384,2560]{1,0:T(8,128)(2,1)}) %all-gather.6.cloned.1.call-update) | async-done | bytes 1966096 | tf_op jit(solution)/shard_map/all_gather | solution.py:73
  49.8 122.7 %all-gather.4.cloned.1.call-done = bf16[384,20480]{1,0:T(8,128)(2,1)} async-done(((bf16[384,1280]{1,0:T(8,128)(2,1)}), bf16[384,20480]{1,0:T(8,128)(2,1)}) %all-gather.4.cloned.1.call-update) | async-done | bytes 15728656 | tf_op jit(solution)/shard_map/all_gather | solution.py:79
  172.5 124.2 %while.14 = (s32[]{:T(128)}, f32[2560,300]{0,1:T(8,128)}, bf16[384,20480]{1,0:T(8,128)(2,1)}, bf16[384,2560]{1,0:T(8,128)(2,1)}, s32[20480]{0:T(1024)S(1)}, /*index=5*/s32[]{:T(128)}, s32[]{:T(128)}, s32[]{:T(128)}, s32[]{:T(128)}) while((s32[]{:T(128)}, f32[2560,300]{0,1:T(8,128)}, bf16[384,20480]{1,0:T(8,128)(2,1)}, ...), condition=%wide.region_4.5_spmd.clone, body=%wide.region_3.4_spmd.clone.sunk | while | flops 35970764800 | bytes 120955040 | solution.py:65
  172.5 37.4 %fusion.clone.9 = bf16[2560,10240]{0,1:T(8,128)(2,1)} fusion(bf16[384,2560]{1,0:T(8,128)(2,1)} %get-tuple-element.184, bf16[384,20480]{1,0:T(8,128)(2,1)} %get-tuple-element.183, s32[]{:T(128)S(6)} %select_n.27), kind=kOutput, calls=%fused_computation.2.clone.clone.clone.clone.clone.2.clone.1 | convolution fusion | flops 20237516800 | bytes 62259204 | tf_op jit(solution)/shard_map/while/body/eval_jaxpr/dot_general | solution.py:44
  209.9 24.2 %fusion.47 = f32[2560,300]{0,1:T(8,128)} fusion(s32[10240]{0:T(1024)S(1)} %dynamic_slice.28, f32[2560,300]{0,1:T(8,128)} %get-tuple-element.173, pred[]{:T(512)S(6)} %compare.3, bf16[2560,10240]{0,1:T(8,128)(2,1)} %fusion.clone.9), kind=kOutput, calls=%fused_computation.7.clone.3 | convolution fusion | flops 15733248000 | bytes 58613760 | tf_op jit(solution)/shard_map/while/body/eval_jaxpr/dot_general | solution.py:52
  234.1 37.4 %fusion.clone.9 = bf16[2560,10240]{0,1:T(8,128)(2,1)} fusion(bf16[384,2560]{1,0:T(8,128)(2,1)} %get-tuple-element.184, bf16[384,20480]{1,0:T(8,128)(2,1)} %get-tuple-element.183, s32[]{:T(128)S(6)} %select_n.27), kind=kOutput, calls=%fused_computation.2.clone.clone.clone.clone.clone.2.clone.1 | convolution fusion | flops 20237516800 | bytes 62259204 | tf_op jit(solution)/shard_map/while/body/eval_jaxpr/dot_general | solution.py:44
  271.6 25.1 %fusion.47 = f32[2560,300]{0,1:T(8,128)} fusion(s32[10240]{0:T(1024)S(1)} %dynamic_slice.28, f32[2560,300]{0,1:T(8,128)} %get-tuple-element.173, pred[]{:T(512)S(6)} %compare.3, bf16[2560,10240]{0,1:T(8,128)(2,1)} %fusion.clone.9), kind=kOutput, calls=%fused_computation.7.clone.3 | convolution fusion | flops 15733248000 | bytes 58613760 | tf_op jit(solution)/shard_map/while/body/eval_jaxpr/dot_general | solution.py:52
  296.7 0.0 reduce-scatter.2.cloned.1.call-update
  296.7 0.7 copy-done.5
  297.4 40.6 %reduce-scatter.2.cloned.1.call-done = f32[1280,300]{0,1:T(8,128)} async-done(((f32[2560,300]{0,1:T(8,128)}), f32[1280,300]{0,1:T(8,128)}) %reduce-scatter.2.cloned.1.call-update) | async-done | bytes 1536016 | tf_op jit(solution)/shard_map/reduce_scatter | solution.py:84
  338.0 1.6 fusion.26
  339.7 0.6 stack.27
  340.3 0.6 stack.28
  340.9 0.6 stack_broadcast_in_dim.3
  341.5 1.4 stack.29
  342.9 2.1 fusion.12
  345.0 39.5 %psum.7 = f32[300,7]{0,1:T(8,128)S(1)} all-reduce(f32[300,7]{0,1:T(8,128)S(1)} %fusion.12), channel_id=1, replica_groups=mesh['genes'=16,'cols'=2] {'genes','cols'}, use_global_device_ids=true, to_apply=%region_8.9 | all-reduce | flops 2100 | bytes 16800 | tf_op jit(solution)/shard_map/psum | solution.py:85
  384.6 0.6 pad_maximum_fusion
  (24 shorter events, 0.1 us)
Async XLA Ops:
  7.2 1.6 copy-start
  7.2 42.6 %all-gather.6.cloned.1.call-start = ((), (), s32[]{:S(2)}) async-start(), calls=%async_computation.2 | async-start | bytes 2949120 | tf_op jit(solution)/shard_map/all_gather | solution.py:73
  11.5 2.1 copy-start.2
  14.0 2.1 copy-start.3
  15.3 157.2 %all-gather.4.cloned.1.call-start = ((), (), s32[]{:S(2)}) async-start(), calls=%async_computation.1 | async-start | bytes 16711680 | tf_op jit(solution)/shard_map/all_gather | solution.py:79
  16.0 322.0 %reduce-scatter.2.cloned.1.call-start = ((), (), s32[]{:S(2)}) async-start(), calls=%async_computation.3 | async-start | bytes 4669440 | tf_op jit(solution)/shard_map/reduce_scatter | solution.py:84
  296.7 0.7 copy-start.5
  296.7 41.4 %copy-start.4 = (s32[1280,300]{0,1:T(8,128)S(1)}, s32[1280,300]{0,1:T(8,128)}, u32[]{:S(2)}) copy-start(s32[1280,300]{0,1:T(8,128)} %param.8) | copy-start | bytes 4608004
  297.4 87.8 %copy-start.1 = (f32[384,1280]{1,0:T(8,128)S(1)}, f32[384,1280]{1,0:T(8,128)}, u32[]{:S(2)}) copy-start(f32[384,1280]{1,0:T(8,128)} %param.6) | copy-start | bytes 5898244
Sparse Core Ops, SparseCore 0:
  15.4 34.3 all-gather.5
  52.6 119.7 all-gather.3
  296.8 41.1 reduce-scatter.1
where the time goes:
time: 392 us
  waiting for transfers between devices  174 us (44%)
  matrix products  126 us (32%)
  blocking collectives  62.8 us (16%)
  between operations  13.9 us (4%)
  other arithmetic  7.47 us (2%)
  local copies, waits for them, and re-layouts  6.83 us (2%)
    all_gather x1, waiting for transfers between devices, local(): lax.all_gather(scaled, 'genes', axis=1, tiled=True)  123 us
    dot_general x2, matrix products, tile_term(): lax.dot_general(row_block, column_block, (((0,), (0,)), ((), ())), prefer...  74.9 us
    dot_general x2, matrix products, tile_term(): return jnp.dot(adjacency, member_block, preferred_element_type=jnp.float32)  49.3 us
    reduce_scatter x1, waiting for transfers between devices, local(): lax.psum_scatter(partial_value, 'cols', scatter_dimension=0, tiled=True)  40.6 us
    psum x1, blocking collectives, local(): lax.psum(local_sums(connectivity, labels, ref_kim), ('genes', 'cols'))  39.5 us
    all_gather x1, blocking collectives, local(): panel_ids = lax.all_gather(module_ids, 'genes', axis=0, tiled=True)  23.3 us
    all_gather x1, waiting for transfers between devices, local(): row_block = lax.all_gather(scaled, 'cols', axis=1, tiled=True)  10.2 us
  transfers between devices with their start and end apart: 3, of which 3 were waited for; matrix products, arithmetic and copies ran while one was open for 0% of the time, Pallas kernels for 0%

commit v1 on v0

--- a/solution.py
+++ b/solution.py
@@ -71,7 +71,14 @@
     shard_width = scaled.shape[1]
     module_ids = jnp.sum(labels * jnp.arange(module_count, dtype=jnp.int32)[None, :], axis=1)
     row_block = lax.all_gather(scaled, "cols", axis=1, tiled=True)
-    panel_ids = lax.all_gather(module_ids, "genes", axis=0, tiled=True)
+    ring = [module_ids]
+    for hop in range(15):
+        ring.append(lax.ppermute(ring[-1], "genes", [(dev, (dev + 1) % 16) for dev in range(16)]))
+    panel_ids = jnp.roll(
+        jnp.concatenate(ring[::-1], axis=0),
+        (lax.axis_index("genes") + 1) * ring[0].shape[0],
+        axis=0,
+    )
     initial = jnp.zeros((row_block.shape[1], module_count), jnp.float32)
     partial_value = add_tiles(
         initial,

time: 392 us -> 393 us (level)
  blocking collectives: 62.8 us -> 39.4 us
  waiting for transfers between devices: 174 us -> 197 us
    ppermute x0 -> x15, waiting for transfers between devices: none -> 89 us  [local(): lax.ppermute(ring[-1], 'genes', [(dev, (dev + 1) % 16) for dev in range(1...]
    all_gather x1, waiting for transfers between devices: 123 us -> 66.5 us  [local(): lax.all_gather(scaled, 'genes', axis=1, tiled=True)]
    all_gather x1 -> x0, blocking collectives: 23.3 us -> none  [local(): panel_ids = lax.all_gather(module_ids, 'genes', axis=0, tiled=True)]
    all_gather x1, waiting for transfers between devices: 10.2 us -> 0.02 us  [local(): row_block = lax.all_gather(scaled, 'cols', axis=1, tiled=True)]
  transfers between devices with their start and end apart: 3 -> 18, of which waited for: 3 -> 17; matrix products, arithmetic and copies ran while one was open for 0% -> 0% of each run, Pallas kernels for 0% -> 0%
where the time goes in v1:
time: 393 us; the launch traced here: 392 us
  waiting for transfers between devices  197 us (50%)
  matrix products  126 us (32%)
  blocking collectives  39.4 us (10%)
  between operations  14.1 us (4%)
  other arithmetic  7.47 us (2%)
  local copies, waits for them, and re-layouts  7.12 us (2%)
    ppermute x15, waiting for transfers between devices, local(): lax.ppermute(ring[-1], 'genes', [(dev, (dev + 1) % 16) for dev in range(1...  89 us
    dot_general x2, matrix products, tile_term(): lax.dot_general(row_block, column_block, (((0,), (0,)), ((), ())), prefer...  74.9 us
    all_gather x1, waiting for transfers between devices, local(): lax.all_gather(scaled, 'genes', axis=1, tiled=True)  66.5 us
    dot_general x2, matrix products, tile_term(): return jnp.dot(adjacency, member_block, preferred_element_type=jnp.float32)  49.4 us
    reduce_scatter x1, waiting for transfers between devices, local(): lax.psum_scatter(partial_value, 'cols', scatter_dimension=0, tiled=True)  40.7 us
    psum x1, blocking collectives, local(): lax.psum(local_sums(connectivity, labels, ref_kim), ('genes', 'cols'))  39.4 us
  transfers between devices with their start and end apart: 18, of which 17 were waited for; matrix products, arithmetic and copies ran while one was open for 0% of the time, Pallas kernels for 0%

profile of v1, /device:TPU:0, one launch (start us, length us, event | category | flops | bytes accessed | tf_op | source)
XLA Modules:
  0.0 392.2 jit_solution(15066444766066820533)
XLA Ops:
  7.2 0.8 compare_select_fusion
  8.0 0.7 compare_and_fusion
  8.8 2.7 gather_fusion
  11.4 1.9 select_reduce_fusion
  14.0 1.3 multiply_convert_fusion
  15.3 0.7 all-gather.3.cloned.1.call-update
  16.8 6.3 %collective-permute-done = s32[1280]{0:T(1024)S(1)} collective-permute-done((s32[1280]{0:T(1024)S(1)}, s32[1280]{0:T(1024)S(1)}, u32[]{:S(2)}, u32[]{:S(2)}) %collective-permute-start) | collective-permute-done | bytes 5152 | tf_op jit(solution)/shard_map/ppermute | solution.py:76
  23.1 5.8 %collective-permute-done.1 = s32[1280]{0:T(1024)S(1)} collective-permute-done((s32[1280]{0:T(1024)S(1)}, s32[1280]{0:T(1024)S(1)}, u32[]{:S(2)}, u32[]{:S(2)}) %collective-permute-start.1) | collective-permute-done | bytes 5152 | tf_op jit(solution)/shard_map/ppermute | solution.py:76
  28.8 5.8 %collective-permute-done.2 = s32[1280]{0:T(1024)S(1)} collective-permute-done((s32[1280]{0:T(1024)S(1)}, s32[1280]{0:T(1024)S(1)}, u32[]{:S(2)}, u32[]{:S(2)}) %collective-permute-start.2) | collective-permute-done | bytes 5152 | tf_op jit(solution)/shard_map/ppermute | solution.py:76
  34.6 5.8 %collective-permute-done.3 = s32[1280]{0:T(1024)S(1)} collective-permute-done((s32[1280]{0:T(1024)S(1)}, s32[1280]{0:T(1024)S(1)}, u32[]{:S(2)}, u32[]{:S(2)}) %collective-permute-start.3) | collective-permute-done | bytes 5152 | tf_op jit(solution)/shard_map/ppermute | solution.py:76
  40.4 5.8 %collective-permute-done.4 = s32[1280]{0:T(1024)S(1)} collective-permute-done((s32[1280]{0:T(1024)S(1)}, s32[1280]{0:T(1024)S(1)}, u32[]{:S(2)}, u32[]{:S(2)}) %collective-permute-start.4) | collective-permute-done | bytes 5152 | tf_op jit(solution)/shard_map/ppermute | solution.py:76
  46.2 5.8 %collective-permute-done.5 = s32[1280]{0:T(1024)S(1)} collective-permute-done((s32[1280]{0:T(1024)S(1)}, s32[1280]{0:T(1024)S(1)}, u32[]{:S(2)}, u32[]{:S(2)}) %collective-permute-start.5) | collective-permute-done | bytes 5152 | tf_op jit(solution)/shard_map/ppermute | solution.py:76
  51.9 5.8 %collective-permute-done.6 = s32[1280]{0:T(1024)S(1)} collective-permute-done((s32[1280]{0:T(1024)S(1)}, s32[1280]{0:T(1024)S(1)}, u32[]{:S(2)}, u32[]{:S(2)}) %collective-permute-start.6) | collective-permute-done | bytes 5152 | tf_op jit(solution)/shard_map/ppermute | solution.py:76
  57.7 5.8 %collective-permute-done.7 = s32[1280]{0:T(1024)S(1)} collective-permute-done((s32[1280]{0:T(1024)S(1)}, s32[1280]{0:T(1024)S(1)}, u32[]{:S(2)}, u32[]{:S(2)}) %collective-permute-start.7) | collective-permute-done | bytes 5152 | tf_op jit(solution)/shard_map/ppermute | solution.py:76
  63.5 6.2 %collective-permute-done.8 = s32[1280]{0:T(1024)S(1)} collective-permute-done((s32[1280]{0:T(1024)S(1)}, s32[1280]{0:T(1024)S(1)}, u32[]{:S(2)}, u32[]{:S(2)}) %collective-permute-start.8) | collective-permute-done | bytes 5152 | tf_op jit(solution)/shard_map/ppermute | solution.py:76
  69.7 6.1 %collective-permute-done.9 = s32[1280]{0:T(1024)S(1)} collective-permute-done((s32[1280]{0:T(1024)S(1)}, s32[1280]{0:T(1024)S(1)}, u32[]{:S(2)}, u32[]{:S(2)}) %collective-permute-start.9) | collective-permute-done | bytes 5152 | tf_op jit(solution)/shard_map/ppermute | solution.py:76
  75.7 6.2 %collective-permute-done.10 = s32[1280]{0:T(1024)S(1)} collective-permute-done((s32[1280]{0:T(1024)S(1)}, s32[1280]{0:T(1024)S(1)}, u32[]{:S(2)}, u32[]{:S(2)}) %collective-permute-start.10) | collective-permute-done | bytes 5152 | tf_op jit(solution)/shard_map/ppermute | solution.py:76
  81.9 6.1 %collective-permute-done.11 = s32[1280]{0:T(1024)S(1)} collective-permute-done((s32[1280]{0:T(1024)S(1)}, s32[1280]{0:T(1024)S(1)}, u32[]{:S(2)}, u32[]{:S(2)}) %collective-permute-start.11) | collective-permute-done | bytes 5152 | tf_op jit(solution)/shard_map/ppermute | solution.py:76
  88.0 6.2 %collective-permute-done.12 = s32[1280]{0:T(1024)S(1)} collective-permute-done((s32[1280]{0:T(1024)S(1)}, s32[1280]{0:T(1024)S(1)}, u32[]{:S(2)}, u32[]{:S(2)}) %collective-permute-start.12) | collective-permute-done | bytes 5152 | tf_op jit(solution)/shard_map/ppermute | solution.py:76
  94.2 5.8 %collective-permute-done.13 = s32[1280]{0:T(1024)S(1)} collective-permute-done((s32[1280]{0:T(1024)S(1)}, s32[1280]{0:T(1024)S(1)}, u32[]{:S(2)}, u32[]{:S(2)}) %collective-permute-start.13) | collective-permute-done | bytes 5152 | tf_op jit(solution)/shard_map/ppermute | solution.py:76
  99.9 5.9 %collective-permute-done.14 = s32[1280]{0:T(1024)S(1)} collective-permute-done((s32[1280]{0:T(1024)S(1)}, s32[1280]{0:T(1024)S(1)}, u32[]{:S(2)}, u32[]{:S(2)}) %collective-permute-start.14) | collective-permute-done | bytes 5152 | tf_op jit(solution)/shard_map/ppermute | solution.py:76
  106.4 66.5 %all-gather.3.cloned.1.call-done = bf16[384,20480]{1,0:T(8,128)(2,1)} async-done(((bf16[384,1280]{1,0:T(8,128)(2,1)}), bf16[384,20480]{1,0:T(8,128)(2,1)}) %all-gather.3.cloned.1.call-update) | async-done | bytes 15728656 | tf_op jit(solution)/shard_map/all_gather | solution.py:86
  172.9 124.3 %while.14 = (s32[]{:T(128)}, f32[2560,300]{0,1:T(8,128)}, bf16[384,20480]{1,0:T(8,128)(2,1)}, bf16[384,2560]{1,0:T(8,128)(2,1)}, s32[20480]{0:T(1024)S(1)}, /*index=5*/s32[]{:T(128)}, s32[]{:T(128)}, s32[]{:T(128)}, s32[]{:T(128)}) while((s32[]{:T(128)}, f32[2560,300]{0,1:T(8,128)}, bf16[384,20480]{1,0:T(8,128)(2,1)}, ...), condition=%wide.region_4.5_spmd.clone, body=%wide.region_3.4_spmd.clone.sunk | while | flops 35970764800 | bytes 120955040 | solution.py:65
  172.9 37.4 %fusion.clone.9 = bf16[2560,10240]{0,1:T(8,128)(2,1)} fusion(bf16[384,2560]{1,0:T(8,128)(2,1)} %get-tuple-element.184, bf16[384,20480]{1,0:T(8,128)(2,1)} %get-tuple-element.183, s32[]{:T(128)S(6)} %select_n.42), kind=kOutput, calls=%fused_computation.2.clone.clone.clone.clone.clone.2.clone.1 | convolution fusion | flops 20237516800 | bytes 62259204 | tf_op jit(solution)/shard_map/while/body/eval_jaxpr/dot_general | solution.py:44
  210.4 24.2 %fusion.47 = f32[2560,300]{0,1:T(8,128)} fusion(s32[10240]{0:T(1024)S(1)} %dynamic_slice.33, f32[2560,300]{0,1:T(8,128)} %get-tuple-element.173, pred[]{:T(512)S(6)} %compare.3, bf16[2560,10240]{0,1:T(8,128)(2,1)} %fusion.clone.9), kind=kOutput, calls=%fused_computation.7.clone.3 | convolution fusion | flops 15733248000 | bytes 58613760 | tf_op jit(solution)/shard_map/while/body/eval_jaxpr/dot_general | solution.py:52
  234.6 37.4 %fusion.clone.9 = bf16[2560,10240]{0,1:T(8,128)(2,1)} fusion(bf16[384,2560]{1,0:T(8,128)(2,1)} %get-tuple-element.184, bf16[384,20480]{1,0:T(8,128)(2,1)} %get-tuple-element.183, s32[]{:T(128)S(6)} %select_n.42), kind=kOutput, calls=%fused_computation.2.clone.clone.clone.clone.clone.2.clone.1 | convolution fusion | flops 20237516800 | bytes 62259204 | tf_op jit(solution)/shard_map/while/body/eval_jaxpr/dot_general | solution.py:44
  272.0 25.1 %fusion.47 = f32[2560,300]{0,1:T(8,128)} fusion(s32[10240]{0:T(1024)S(1)} %dynamic_slice.33, f32[2560,300]{0,1:T(8,128)} %get-tuple-element.173, pred[]{:T(512)S(6)} %compare.3, bf16[2560,10240]{0,1:T(8,128)(2,1)} %fusion.clone.9), kind=kOutput, calls=%fused_computation.7.clone.3 | convolution fusion | flops 15733248000 | bytes 58613760 | tf_op jit(solution)/shard_map/while/body/eval_jaxpr/dot_general | solution.py:52
  297.9 40.7 %reduce-scatter.2.cloned.1.call-done = f32[1280,300]{0,1:T(8,128)} async-done(((f32[2560,300]{0,1:T(8,128)}), f32[1280,300]{0,1:T(8,128)}) %reduce-scatter.2.cloned.1.call-update) | async-done | bytes 1536016 | tf_op jit(solution)/shard_map/reduce_scatter | solution.py:91
  338.6 1.6 fusion.26
  342.1 1.4 stack.29
  343.4 2.1 fusion.12
  345.6 39.4 %psum.7 = f32[300,7]{0,1:T(8,128)S(1)} all-reduce(f32[300,7]{0,1:T(8,128)S(1)} %fusion.12), channel_id=1, replica_groups=mesh['genes'=16,'cols'=2] {'genes','cols'}, use_global_device_ids=true, to_apply=%region_8.9 | all-reduce | flops 2100 | bytes 16800 | tf_op jit(solution)/shard_map/psum | solution.py:92
  (86 shorter events, 5.0 us)
Async XLA Ops:
  7.2 1.6 copy-start
  7.2 99.2 %all-gather.5.cloned.1.call-start = ((), (), s32[]{:S(2)}) async-start(), calls=%async_computation.2 | async-start | bytes 2949120 | tf_op jit(solution)/shard_map/all_gather | solution.py:73
  11.4 2.1 copy-start.2
  13.9 2.1 copy-start.3
  15.2 157.7 %all-gather.3.cloned.1.call-start = ((), (), s32[]{:S(2)}) async-start(), calls=%async_computation.1 | async-start | bytes 16711680 | tf_op jit(solution)/shard_map/all_gather | solution.py:86
  16.0 322.6 %reduce-scatter.2.cloned.1.call-start = ((), (), s32[]{:S(2)}) async-start(), calls=%async_computation.3 | async-start | bytes 4669440 | tf_op jit(solution)/shard_map/reduce_scatter | solution.py:91
  16.2 6.9 %collective-permute-start = (s32[1280]{0:T(1024)S(1)}, s32[1280]{0:T(1024)S(1)}, u32[]{:S(2)}, u32[]{:S(2)}) collective-permute-start(s32[1280]{0:T(1024)S(1)} %multiply_reduce_fusion.2), channel_id=1, source_target_pairs={{0,2},{2,4},{4,6},{6,8},{8,10},{10,12},{12,14},{14,16},{16,18},{18... | collective-permute-start | bytes 15368 | tf_op jit(solution)/shard_map/ppermute | solution.py:76
  23.1 5.8 %collective-permute-start.1 = (s32[1280]{0:T(1024)S(1)}, s32[1280]{0:T(1024)S(1)}, u32[]{:S(2)}, u32[]{:S(2)}) collective-permute-start(s32[1280]{0:T(1024)S(1)} %collective-permute-done), channel_id=1, source_target_pairs={{0,2},{2,4},{4,6},{6,8},{8,10},{10,12},{12,14},{14,16},{16,18},{18... | collective-permute-start | bytes 15368 | tf_op jit(solution)/shard_map/ppermute | solution.py:76
  28.8 5.8 %collective-permute-start.2 = (s32[1280]{0:T(1024)S(1)}, s32[1280]{0:T(1024)S(1)}, u32[]{:S(2)}, u32[]{:S(2)}) collective-permute-start(s32[1280]{0:T(1024)S(1)} %collective-permute-done.1), channel_id=1, source_target_pairs={{0,2},{2,4},{4,6},{6,8},{8,10},{10,12},{12,14},{14,16},{16,18},{18... | collective-permute-start | bytes 15368 | tf_op jit(solution)/shard_map/ppermute | solution.py:76
  34.6 5.8 %collective-permute-start.3 = (s32[1280]{0:T(1024)S(1)}, s32[1280]{0:T(1024)S(1)}, u32[]{:S(2)}, u32[]{:S(2)}) collective-permute-start(s32[1280]{0:T(1024)S(1)} %collective-permute-done.2), channel_id=1, source_target_pairs={{0,2},{2,4},{4,6},{6,8},{8,10},{10,12},{12,14},{14,16},{16,18},{18... | collective-permute-start | bytes 15368 | tf_op jit(solution)/shard_map/ppermute | solution.py:76
  40.4 5.8 %collective-permute-start.4 = (s32[1280]{0:T(1024)S(1)}, s32[1280]{0:T(1024)S(1)}, u32[]{:S(2)}, u32[]{:S(2)}) collective-permute-start(s32[1280]{0:T(1024)S(1)} %collective-permute-done.3), channel_id=1, source_target_pairs={{0,2},{2,4},{4,6},{6,8},{8,10},{10,12},{12,14},{14,16},{16,18},{18... | collective-permute-start | bytes 15368 | tf_op jit(solution)/shard_map/ppermute | solution.py:76
  46.2 5.8 %collective-permute-start.5 = (s32[1280]{0:T(1024)S(1)}, s32[1280]{0:T(1024)S(1)}, u32[]{:S(2)}, u32[]{:S(2)}) collective-permute-start(s32[1280]{0:T(1024)S(1)} %collective-permute-done.4), channel_id=1, source_target_pairs={{0,2},{2,4},{4,6},{6,8},{8,10},{10,12},{12,14},{14,16},{16,18},{18... | collective-permute-start | bytes 15368 | tf_op jit(solution)/shard_map/ppermute | solution.py:76
  51.9 5.8 %collective-permute-start.6 = (s32[1280]{0:T(1024)S(1)}, s32[1280]{0:T(1024)S(1)}, u32[]{:S(2)}, u32[]{:S(2)}) collective-permute-start(s32[1280]{0:T(1024)S(1)} %collective-permute-done.5), channel_id=1, source_target_pairs={{0,2},{2,4},{4,6},{6,8},{8,10},{10,12},{12,14},{14,16},{16,18},{18... | collective-permute-start | bytes 15368 | tf_op jit(solution)/shard_map/ppermute | solution.py:76
  57.7 5.8 %collective-permute-start.7 = (s32[1280]{0:T(1024)S(1)}, s32[1280]{0:T(1024)S(1)}, u32[]{:S(2)}, u32[]{:S(2)}) collective-permute-start(s32[1280]{0:T(1024)S(1)} %collective-permute-done.6), channel_id=1, source_target_pairs={{0,2},{2,4},{4,6},{6,8},{8,10},{10,12},{12,14},{14,16},{16,18},{18... | collective-permute-start | bytes 15368 | tf_op jit(solution)/shard_map/ppermute | solution.py:76
  63.5 6.2 %collective-permute-start.8 = (s32[1280]{0:T(1024)S(1)}, s32[1280]{0:T(1024)S(1)}, u32[]{:S(2)}, u32[]{:S(2)}) collective-permute-start(s32[1280]{0:T(1024)S(1)} %collective-permute-done.7), channel_id=1, source_target_pairs={{0,2},{2,4},{4,6},{6,8},{8,10},{10,12},{12,14},{14,16},{16,18},{18... | collective-permute-start | bytes 15368 | tf_op jit(solution)/shard_map/ppermute | solution.py:76
  69.7 6.1 %collective-permute-start.9 = (s32[1280]{0:T(1024)S(1)}, s32[1280]{0:T(1024)S(1)}, u32[]{:S(2)}, u32[]{:S(2)}) collective-permute-start(s32[1280]{0:T(1024)S(1)} %collective-permute-done.8), channel_id=1, source_target_pairs={{0,2},{2,4},{4,6},{6,8},{8,10},{10,12},{12,14},{14,16},{16,18},{18... | collective-permute-start | bytes 15368 | tf_op jit(solution)/shard_map/ppermute | solution.py:76
  75.7 6.2 %collective-permute-start.10 = (s32[1280]{0:T(1024)S(1)}, s32[1280]{0:T(1024)S(1)}, u32[]{:S(2)}, u32[]{:S(2)}) collective-permute-start(s32[1280]{0:T(1024)S(1)} %collective-permute-done.9), channel_id=1, source_target_pairs={{0,2},{2,4},{4,6},{6,8},{8,10},{10,12},{12,14},{14,16},{16,18},{18... | collective-permute-start | bytes 15368 | tf_op jit(solution)/shard_map/ppermute | solution.py:76
  81.9 6.1 %collective-permute-start.11 = (s32[1280]{0:T(1024)S(1)}, s32[1280]{0:T(1024)S(1)}, u32[]{:S(2)}, u32[]{:S(2)}) collective-permute-start(s32[1280]{0:T(1024)S(1)} %collective-permute-done.10), channel_id=1, source_target_pairs={{0,2},{2,4},{4,6},{6,8},{8,10},{10,12},{12,14},{14,16},{16,18},{18... | collective-permute-start | bytes 15368 | tf_op jit(solution)/shard_map/ppermute | solution.py:76
  88.0 6.2 %collective-permute-start.12 = (s32[1280]{0:T(1024)S(1)}, s32[1280]{0:T(1024)S(1)}, u32[]{:S(2)}, u32[]{:S(2)}) collective-permute-start(s32[1280]{0:T(1024)S(1)} %collective-permute-done.11), channel_id=1, source_target_pairs={{0,2},{2,4},{4,6},{6,8},{8,10},{10,12},{12,14},{14,16},{16,18},{18... | collective-permute-start | bytes 15368 | tf_op jit(solution)/shard_map/ppermute | solution.py:76
  94.2 5.8 %collective-permute-start.13 = (s32[1280]{0:T(1024)S(1)}, s32[1280]{0:T(1024)S(1)}, u32[]{:S(2)}, u32[]{:S(2)}) collective-permute-start(s32[1280]{0:T(1024)S(1)} %collective-permute-done.12), channel_id=1, source_target_pairs={{0,2},{2,4},{4,6},{6,8},{8,10},{10,12},{12,14},{14,16},{16,18},{18... | collective-permute-start | bytes 15368 | tf_op jit(solution)/shard_map/ppermute | solution.py:76
  99.9 5.9 %collective-permute-start.14 = (s32[1280]{0:T(1024)S(1)}, s32[1280]{0:T(1024)S(1)}, u32[]{:S(2)}, u32[]{:S(2)}) collective-permute-start(s32[1280]{0:T(1024)S(1)} %collective-permute-done.13), channel_id=1, source_target_pairs={{0,2},{2,4},{4,6},{6,8},{8,10},{10,12},{12,14},{14,16},{16,18},{18... | collective-permute-start | bytes 15368 | tf_op jit(solution)/shard_map/ppermute | solution.py:76
  297.2 0.7 copy-start.5
  297.2 41.4 %copy-start.4 = (s32[1280,300]{0,1:T(8,128)S(1)}, s32[1280,300]{0,1:T(8,128)}, u32[]{:S(2)}) copy-start(s32[1280,300]{0,1:T(8,128)} %param.8) | copy-start | bytes 4608004
  297.9 87.8 %copy-start.1 = (f32[384,1280]{1,0:T(8,128)S(1)}, f32[384,1280]{1,0:T(8,128)}, u32[]{:S(2)}) copy-start(f32[384,1280]{1,0:T(8,128)} %param.6) | copy-start | bytes 5898244
Sparse Core Ops, SparseCore 0:
  15.4 34.3 all-gather.4
  52.6 120.2 all-gather.2
  297.3 41.1 reduce-scatter.1
